TPU v7x, 32 devices: a whole 2x2x4 slice. The times are simulated.
32 devices in a mesh: comp: 2 (over x), gy: 4 (over z), gx: 4 (over y, core).
Axes of the slice: x: 2, y: 2, z: 4, core: 2. Of those that a mesh axis runs over, the one named last changes fastest.
Arguments:
- column_water: float32 [2, 16, 32, 512], P('comp', None, 'gy', 'gx'), may hold values from 0.2 to 2
- land_soil: float32 [2, 32, 512], P('comp', 'gy', 'gx'), may hold values from 0.1 to 0.9
- level_weight: float32 [16], replicated, may hold values from 0.01 to 0.1
- excess_weight: float32 [16], replicated, may hold values from 0.3 to 3
- soil_weight: float32 [16], replicated, may hold values from 0.3 to 3
- terrain_class: int32 [320, 5120], P('gy', 'gx'), may hold values from 0 to 15
- surface_head: float32 [2, 320, 5120], P('comp', 'gy', 'gx'), may hold values from 0 to 1
- conductivity: float32 [2, 320, 5120], P('comp', 'gy', 'gx'), may hold values from 0.02 to 0.22
- active_mask: int32 [2, 320, 5120], P('comp', 'gy', 'gx'), may hold values 0 or 1
- flow_code: int32 [2, 320, 5120], P('comp', 'gy', 'gx'), may hold values from 0 to 3
Outputs:
- coupled_state: float32 [2, 32, 512], P('comp', 'gy', 'gx')
All inputs are finite; a program needn't handle non-finite values. No bound on the sum of `active_mask` on one device may be relied on, other than what follows from the above.
Results may differ from a plain program's by a relative error of at most 0.0003.
Values sent between devices are 32-bit elements; how exact they have to be, the bound alone decides.
A program may use at most 64 MiB of HBM per device.

v0:
```python
import functools

import jax
import jax.numpy as jnp
from jax import lax
from jax.experimental import pallas as pl
from jax.experimental.pallas import tpu as pltpu
from jax.sharding import PartitionSpec as P

AGG = 10
NSUB = 8
SWEEPS = 2

diffusion_rate = 0.2
infiltration_rate = 0.05
drainage_rate = 0.1
half_point = 0.1
evaporation_scale = 0.5

LANE = 128
SUB = 8
MESH = pl.DeviceIdType.MESH
DIRS = ((-1, 0), (1, 0), (0, -1), (0, 1), (-1, -1), (-1, 1), (1, -1), (1, 1))
N, S, W, E, NW, NE, SW, SE = range(8)
OPP = (S, N, E, W, SE, SW, NE, NW)


def iota(shape, dim):
    return lax.broadcasted_iota(jnp.int32, shape, dim)


def pick(table, classes):
    values = [table[k] for k in range(table.shape[0])]
    bit = 1
    while len(values) > 1:
        odd = (classes & bit) != 0
        values = [
            jnp.where(odd, values[k + 1], values[k]) for k in range(0, len(values), 2)
        ]
        bit *= 2
    return values[0]


def halves(x):
    high = x.astype(jnp.bfloat16)
    return high, (x - high.astype(jnp.float32)).astype(jnp.bfloat16)


def kernel(
    ny, nx,
    lw, ewt, swt, water_in, soil_in, terrain_in, head_in, cond_in, active_in, code_in,
    out_ref,
    xi, xf, st, ps, wb, mb, pk, dg, mn, qb, qx, back_tx, back_rx, gather, spreadm,
    send, recv, local, hop,
):
    group = lax.axis_index("comp")
    gy = lax.axis_index("gy")
    gx = lax.axis_index("gx")
    rows, cols = terrain_in.shape
    lev = water_in.shape[1]
    crow, ccol = soil_in.shape[1], soil_in.shape[2]
    tiles = cols // LANE
    width = tiles + 1
    bands = rows // SUB + 2

    lane = iota((SUB, LANE), 1)
    sub = iota((SUB, LANE), 0)

    def exists(d):
        dy, dx = DIRS[d]
        return (gy + dy >= 0) & (gy + dy < ny) & (gx + dx >= 0) & (gx + dx < nx)

    def at(d):
        dy, dx = DIRS[d]
        return {"comp": group, "gy": gy + dy, "gx": gx + dx}

    partner = {"comp": 1 - group, "gy": gy, "gx": gx}

    def copy(src, dst, d, f):
        return pltpu.make_async_remote_copy(
            src_ref=src, dst_ref=dst, send_sem=send.at[d, f], recv_sem=recv.at[OPP[d], f],
            device_id=at(d), device_id_type=MESH,
        )

    def arrival(dst, d, f):
        return pltpu.make_async_remote_copy(
            src_ref=dst, dst_ref=dst, send_sem=send.at[d, f], recv_sem=recv.at[d, f],
            device_id=at(d), device_id_type=MESH,
        )

    fields = (
        (cond_in.at[0], xf.at[0]),
        (active_in.at[0], xi.at[1]),
        (code_in.at[0], xi.at[2]),
        (head_in.at[0], xf.at[1]),
        (terrain_in, xi.at[0]),
    )
    rfrom = {-1: (0, SUB), 0: (0, rows), 1: (rows - SUB, SUB)}
    cfrom = {-1: (0, LANE), 0: (0, cols), 1: (cols - LANE, LANE)}
    rslot = {-1: (0, SUB), 0: (SUB, rows), 1: (rows + SUB, SUB)}
    cslot = {-1: (cols + LANE, LANE), 0: (0, cols), 1: (cols, LANE)}

    def cut(ref, r, c):
        return ref.at[pl.ds(r[0], r[1]), pl.ds(c[0], c[1])]

    def part(ref, d):
        return cut(ref, rfrom[DIRS[d][0]], cfrom[DIRS[d][1]])

    def slot(ref, d):
        return cut(ref, rslot[DIRS[d][0]], cslot[DIRS[d][1]])

    own = ((SUB, rows), (0, cols))

    def local_copy(src, dst, k):
        return pltpu.make_async_copy(src, dst, local.at[k])

    terrain_load = local_copy(terrain_in, cut(xi.at[0], *own), 4)
    route_loads = [local_copy(f[0], cut(f[1], *own), k) for k, f in enumerate(fields[:4])]
    water_load = local_copy(water_in.at[0], wb.at[8], 0)
    soil_load = local_copy(soil_in.at[0], mb.at[8], 1)

    barrier = pltpu.get_barrier_semaphore()
    for d in range(8):
        @pl.when(exists(d))
        def _():
            pl.semaphore_signal(barrier, inc=1, device_id=at(d), device_id_type=MESH)
    pl.semaphore_signal(barrier, inc=1, device_id=partner, device_id_type=MESH)
    greeted = 1
    for d in range(8):
        greeted = greeted + exists(d).astype(jnp.int32)

    terrain_load.start()

    @pl.when(group == 0)
    def _():
        water_load.start()
        soil_load.start()

    @pl.when(group == 1)
    def _():
        for load in route_loads:
            load.start()

    pl.semaphore_wait(barrier, greeted)

    def land_first(d):
        out = [copy(soil_in.at[0], mb.at[OPP[d]], d, 1)]
        if d < 4:
            out.insert(0, copy(water_in.at[0], wb.at[OPP[d]], d, 0))
        return out

    def land_pack(d):
        return copy(pk.at[0 if DIRS[d][1] < 0 else 1], dg.at[OPP[d] - 4], d, 0)

    def land_mean(d):
        return copy(mn.at[8], mn.at[OPP[d]], d, 2)

    def route_sends(d):
        return [copy(part(f[0], d), slot(f[1], OPP[d]), d, k) for k, f in enumerate(fields)]

    q_send = pltpu.make_async_remote_copy(
        src_ref=qb.at[0], dst_ref=qb.at[1], send_sem=hop.at[0], recv_sem=hop.at[1],
        device_id=partner, device_id_type=MESH,
    )
    back_send = pltpu.make_async_remote_copy(
        src_ref=back_tx, dst_ref=back_rx, send_sem=hop.at[2], recv_sem=hop.at[3],
        device_id=partner, device_id_type=MESH,
    )

    def over(dirs, act):
        for d in dirs:
            @pl.when(exists(d))
            def _():
                act(d)

    def start_all(copies):
        for c in copies:
            c.start()

    @pl.when(group == 0)
    def _():
        over(range(8), lambda d: start_all(land_first(d)))

    @pl.when(group == 1)
    def _():
        over(range(8), lambda d: start_all(route_sends(d)))

    k10 = iota((LANE, ccol), 1) * AGG
    j0 = iota((LANE, ccol), 0)

    for c in range(tiles):
        j = j0 + c * LANE
        gather[c * LANE : (c + 1) * LANE, :] = jnp.where(
            (j >= k10) & (j < k10 + AGG), 1.0, 0.0
        ).astype(jnp.bfloat16)

    def means(first, second):
        parts = []
        for field in (first, second):
            high, low = [], []
            for tile in field:
                a, b = halves(tile)
                high.append(a)
                low.append(b)
            parts.append(jnp.concatenate(high, axis=1))
            parts.append(jnp.concatenate(low, axis=1))
        stacked = jnp.concatenate(parts, axis=0)
        y = jnp.dot(stacked, gather[...], preferred_element_type=jnp.float32)
        i10 = iota((crow, rows), 0) * AGG
        i = iota((crow, rows), 1)
        pool = jnp.where((i >= i10) & (i < i10 + AGG), 1.0, 0.0)
        total = []
        for k in (0, 2):
            z = y[k * rows : (k + 1) * rows] + y[(k + 1) * rows : (k + 2) * rows]
            total.append(
                jnp.dot(pool, z, preferred_element_type=jnp.float32, precision=lax.Precision.HIGHEST)
                * (1.0 / (AGG * AGG))
            )
        return total

    @pl.when(group == 0)
    def _():
        water_load.wait()
        packs = [jnp.zeros((SUB, LANE), jnp.float32), jnp.zeros((SUB, LANE), jnp.float32)]
        for l in range(lev):
            mine = (lane >= 8 * l) & (lane < 8 * l + 8)
            w = wb[8, l]
            packs[0] = jnp.where(mine, pltpu.roll(w, (8 * l) % LANE, 1), packs[0])
            packs[1] = jnp.where(mine, pltpu.roll(w, (8 * l + 8) % LANE, 1), packs[1])
        pk[0] = packs[0]
        pk[1] = packs[1]
        over(range(4, 8), lambda d: land_pack(d).start())

        terrain_load.wait()
        firsts, seconds = [], []
        for c in range(tiles):
            tc = xi[0, SUB : SUB + rows, c * LANE : (c + 1) * LANE]
            firsts.append(pick(ewt, tc))
            seconds.append(pick(swt, tc))
        mean_e, mean_s = means(firsts, seconds)
        mn[8, 0] = mean_e
        mn[8, 1] = mean_s
        over(range(8), lambda d: land_mean(d).start())

        soil_load.wait()
        over(range(4), lambda d: arrival(wb.at[d], d, 0).wait_recv())
        over(range(4, 8), lambda d: arrival(dg.at[d - 4], d, 0).wait_recv())
        over(range(8), lambda d: arrival(mb.at[d], d, 1).wait_recv())

        def valid(a, b):
            r = sub + (0 if a == 0 else jnp.where(sub < 4, crow, -crow))
            r = r + gy * crow
            k = lane + (0 if b == 0 else jnp.where(lane < 64, ccol, -ccol))
            k = k + gx * ccol
            return (r >= 0) & (r < ny * crow) & (k >= 0) & (k < nx * ccol)

        ok = [[valid(a, b) for b in range(2)] for a in range(2)]
        left = lane < 64
        upper = sub < 4

        def joined(get, corner, fill):
            t = [
                [get(8), jnp.where(left, get(E), get(W))],
                [jnp.where(upper, get(S), get(N)), corner],
            ]
            return [[jnp.where(ok[a][b], t[a][b], fill) for b in range(2)] for a in range(2)]

        def corners(get):
            return jnp.where(
                upper,
                jnp.where(left, get(SE), get(SW)),
                jnp.where(left, get(NE), get(NW)),
            )

        def smooth(t):
            new = [[None, None], [None, None]]
            down = [[pltpu.roll(t[a][b], 1, 0) for b in range(2)] for a in range(2)]
            up = [[pltpu.roll(t[a][b], SUB - 1, 0) for b in range(2)] for a in range(2)]
            right = [[pltpu.roll(t[a][b], 1, 1) for b in range(2)] for a in range(2)]
            lft = [[pltpu.roll(t[a][b], LANE - 1, 1) for b in range(2)] for a in range(2)]
            for a in range(2):
                for b in range(2):
                    around = (
                        jnp.where(sub == 0, down[1 - a][b], down[a][b])
                        + jnp.where(sub == SUB - 1, up[1 - a][b], up[a][b])
                        + jnp.where(lane == 0, right[a][1 - b], right[a][b])
                        + jnp.where(lane == LANE - 1, lft[a][1 - b], lft[a][b])
                    )
                    value = t[a][b] + diffusion_rate * (around - 4.0 * t[a][b])
                    new[a][b] = jnp.where(ok[a][b], value, 0.0)
            return new

        ce = jnp.where(upper, dg[SE - 4], dg[NE - 4])
        cw = jnp.where(upper, dg[SW - 4], dg[NW - 4])
        precip = [[0.0, 0.0], [0.0, 0.0]]
        ground = None
        for l in range(lev):
            corner = jnp.where(
                left,
                pltpu.roll(ce, (LANE - 8 * l) % LANE, 1),
                pltpu.roll(cw, (2 * LANE - 8 - 8 * l) % LANE, 1),
            )
            t = joined(lambda k: wb[k, l], corner, 0.0)
            for _ in range(SWEEPS):
                t = smooth(t)
            if l == 0:
                ground = t[0][0]
            for a in range(2):
                for b in range(2):
                    precip[a][b] = precip[a][b] + lw[l] * t[a][b] * t[a][b]

        moisture = joined(lambda k: mb[k], corners(lambda k: mb[k]), 0.5)
        over(range(8), lambda d: arrival(mn.at[d], d, 2).wait_recv())
        m_e = joined(lambda k: mn[k, 0], corners(lambda k: mn[k, 0]), 1.0)
        m_s = joined(lambda k: mn[k, 1], corners(lambda k: mn[k, 1]), 1.0)
        for a in range(2):
            for b in range(2):
                m = moisture[a][b]
                excess = precip[a][b] * m * m / (m * m + half_point)
                rs = slice(a * SUB, (a + 1) * SUB)
                cs = slice(b * LANE, (b + 1) * LANE)
                qb[0, 0, rs, cs] = excess / m_e[a][b]
                qb[0, 1, rs, cs] = m / m_s[a][b]
        q_send.start()
        divisor = 1.0 + evaporation_scale * ground * ground
        over(range(8), lambda d: [c.wait_send() for c in land_first(d)])
        over(range(4, 8), lambda d: land_pack(d).wait_send())
        over(range(8), lambda d: land_mean(d).wait_send())
        q_send.wait_send()
        back_send.wait_recv()
        out_ref[0] = back_rx[...] / divisor

    R, AD, M0, M1, M2, M3, EW, HD, SO = range(9)
    WN, WS, WW, WE, AA, B0, B1, B2, B3 = range(9, 18)

    @pl.when(group == 1)
    def _():
        kk = iota((2 * ccol, LANE), 0)
        jj = iota((2 * ccol, LANE), 1)
        for c in range(tiles):
            j = jj + c * LANE
            spreadm[:, c * LANE : (c + 1) * LANE] = jnp.where(
                (j >= kk * AGG) & (j < kk * AGG + AGG), 1.0, 0.0
            ).astype(jnp.bfloat16)
        spreadm[:, cols:] = jnp.where(
            ((jj < 64) & (kk == ccol)) | ((jj >= 64) & (kk == 2 * ccol - 1)), 1.0, 0.0
        ).astype(jnp.bfloat16)

        zero = jnp.zeros((SUB, LANE), jnp.float32)
        for c in range(width):
            for edge in (0, (bands + 1) * SUB):
                for k in (R, M0, M1):
                    st[k, c, edge : edge + SUB] = zero
                for k in range(2):
                    for p in range(2):
                        ps[p, k, c, edge : edge + SUB] = zero

        def prepare(t, c):
            r = pl.ds(t * SUB if isinstance(t, int) else pl.multiple_of(t * SUB, SUB), SUB)
            o = pl.ds(
                (t + 1) * SUB if isinstance(t, int) else pl.multiple_of(t * SUB + SUB, SUB), SUB
            )

            def take(ref, k):
                a = ref[k, r, c * LANE : (c + 1) * LANE]
                if c < tiles:
                    return a
                return jnp.where(lane < 64, a, ref[k, r, (c + 1) * LANE : (c + 2) * LANE])

            row = sub + (t - 1) * SUB + gy * rows
            col = lane + c * LANE
            if c == tiles:
                col = jnp.where(lane < 64, col, lane - LANE)
            col = col + gx * cols
            ok = (row >= 0) & (row < ny * rows) & (col >= 0) & (col < nx * cols)
            active = jnp.where(ok, take(xi, 1).astype(jnp.float32), 0.0)
            code = take(xi, 2)
            keff = jnp.where(ok, take(xf, 0), 0.0) * active
            tc = take(xi, 0)
            st[R, c, o] = jnp.sqrt(keff)
            rate = drainage_rate * active
            st[AD, c, o] = rate
            for k in range(4):
                st[M0 + k, c, o] = jnp.where(code == k, rate, 0.0)
            st[EW, c, o] = active * pick(ewt, tc)
            st[HD, c, o] = active * jnp.where(ok, take(xf, 1), 0.0)
            st[SO, c, o] = pick(swt, tc)

        for load in route_loads:
            load.wait()
        terrain_load.wait()

        def inner(t, carry):
            for c in range(tiles):
                prepare(t, c)
            return carry

        lax.fori_loop(1, bands - 1, inner, 0, unroll=2)

        over(range(8), lambda d: [arrival(slot(f[1], d), d, k).wait_recv() for k, f in enumerate(fields)])

        def rim(k, carry):
            for c in range(tiles):
                prepare(k * (bands - 1), c)
            return carry

        lax.fori_loop(0, 2, rim, 0)

        def side(t, carry):
            prepare(t, tiles)
            return carry

        lax.fori_loop(0, bands, side, 0, unroll=6)

        def from_west(tile_list):
            turned = [pltpu.roll(x, 1, 1) for x in tile_list]
            return [jnp.where(lane == 0, turned[c - 1], turned[c]) for c in range(width)]

        def from_east(tile_list):
            turned = [pltpu.roll(x, LANE - 1, 1) for x in tile_list]
            return [
                jnp.where(lane == LANE - 1, turned[(c + 1) % width], turned[c])
                for c in range(width)
            ]

        def couple(t, carry):
            base = pl.multiple_of(t * SUB + SUB, SUB)
            o = pl.ds(base, SUB)
            above = pl.ds(base - 1, SUB)
            below = pl.ds(base + 1, SUB)
            r = [st[R, c, o] for c in range(width)]
            west, east = from_west(r), from_east(r)
            for c in range(width):
                wn = r[c] * st[R, c, above]
                ws = r[c] * st[R, c, below]
                ww = r[c] * west[c]
                we = r[c] * east[c]
                st[WN, c, o] = wn
                st[WS, c, o] = ws
                st[WW, c, o] = ww
                st[WE, c, o] = we
                st[AA, c, o] = (wn + ws) + (ww + we)
                st[B0, c, o] = st[M0, c, below]
                st[B1, c, o] = st[M1, c, above]
            for c, v in enumerate(from_east([st[M2, c, o] for c in range(width)])):
                st[B2, c, o] = v
            for c, v in enumerate(from_west([st[M3, c, o] for c in range(width)])):
                st[B3, c, o] = v
            return carry

        lax.fori_loop(0, bands, couple, 0, unroll=4)

        q_send.wait_recv()
        high, low = [], []
        for k in range(2):
            a, b = halves(qb[1, k])
            high.append(a)
            low.append(b)
        y = jnp.dot(
            jnp.concatenate(high + low, axis=0), spreadm[...], preferred_element_type=jnp.float32
        )
        qx[...] = y[: 4 * SUB] + y[4 * SUB :]
        for t in range(bands):
            o = slice((t + 1) * SUB, (t + 2) * SUB)
            if t == 0:
                a = b = 2 * crow - 1
            elif t == bands - 1:
                a = b = crow
            else:
                a, b = ((t - 1) * SUB) // AGG, ((t - 1) * SUB + SUB - 1) // AGG
            for c in range(width):
                cs = slice(c * LANE, (c + 1) * LANE)

                def up(k):
                    first = jnp.broadcast_to(qx[k * 16 + a : k * 16 + a + 1, cs], (SUB, LANE))
                    if a == b:
                        return first
                    second = jnp.broadcast_to(qx[k * 16 + b : k * 16 + b + 1, cs], (SUB, LANE))
                    return jnp.where(sub < b * AGG - (t - 1) * SUB, first, second)

                ps[0, 0, c, o] = st[HD, c, o] + st[EW, c, o] * up(0)
                ps[0, 1, c, o] = st[SO, c, o] * up(1)

        def substep(src, dst):
            def band(t, carry):
                base = pl.multiple_of(t * SUB + SUB, SUB)
                o = pl.ds(base, SUB)
                above = pl.ds(base - 1, SUB)
                below = pl.ds(base + 1, SUB)
                p = [ps[src, 0, c, o] for c in range(width)]
                s = [ps[src, 1, c, o] for c in range(width)]
                ss = [x * x for x in s]
                p_w, p_e = from_west(p), from_east(p)
                s_w, s_e = from_west(ss), from_east(ss)
                for c in range(width):
                    s_n = ps[src, 1, c, above]
                    s_s = ps[src, 1, c, below]
                    spread = (
                        st[WN, c, o] * ps[src, 0, c, above]
                        + st[WS, c, o] * ps[src, 0, c, below]
                        + (st[WW, c, o] * p_w[c] + st[WE, c, o] * p_e[c])
                        - st[AA, c, o] * p[c]
                    )
                    soaked = infiltration_rate * p[c] * pl.reciprocal(1.0 + s[c])
                    inflow = (
                        st[B0, c, o] * (s_s * s_s)
                        + st[B1, c, o] * (s_n * s_n)
                        + (st[B2, c, o] * s_e[c] + st[B3, c, o] * s_w[c])
                        - st[AD, c, o] * ss[c]
                    )
                    ps[dst, 0, c, o] = p[c] + (spread - soaked)
                    ps[dst, 1, c, o] = s[c] + (soaked + inflow)
                return carry

            lax.fori_loop(0, bands, band, 0, unroll=12)

        def two(k, carry):
            substep(0, 1)
            substep(1, 0)
            return carry

        lax.fori_loop(0, NSUB // 2, two, 0)

        inside = slice(2 * SUB, 2 * SUB + rows)
        mean_p, mean_st = means(
            [ps[0, 0, c, inside] for c in range(tiles)],
            [ps[0, 1, c, inside] for c in range(tiles)],
        )
        back_tx[...] = mean_st
        back_send.start()
        out_ref[0] = mean_p
        over(range(8), lambda d: [c.wait_send() for c in route_sends(d)])
        back_send.wait_send()


def per_device(ny, nx, column_water, land_soil, level_weight, excess_weight, soil_weight,
               terrain_class, surface_head, conductivity, active_mask, flow_code):
    rows, cols = terrain_class.shape
    lev = column_water.shape[1]
    crow, ccol = land_soil.shape[1:]
    wide = cols // LANE + 1
    tall = rows + 4 * SUB
    f32, i32 = jnp.float32, jnp.int32
    any_spec = pl.BlockSpec(memory_space=pltpu.HBM)
    smem = pl.BlockSpec(memory_space=pltpu.SMEM)
    return pl.pallas_call(
        functools.partial(kernel, ny, nx),
        out_shape=jax.ShapeDtypeStruct((1, crow, ccol), f32),
        in_specs=[smem] * 3 + [any_spec] * 7,
        out_specs=pl.BlockSpec(memory_space=pltpu.VMEM),
        scratch_shapes=[
            pltpu.VMEM((3, rows + 2 * SUB, cols + 2 * LANE), i32),
            pltpu.VMEM((2, rows + 2 * SUB, cols + 2 * LANE), f32),
            pltpu.VMEM((18, wide, tall, LANE), f32),
            pltpu.VMEM((2, 2, wide, tall, LANE), f32),
            pltpu.VMEM((9, lev, crow, ccol), f32),
            pltpu.VMEM((9, crow, ccol), f32),
            pltpu.VMEM((2, crow, ccol), f32),
            pltpu.VMEM((4, crow, ccol), f32),
            pltpu.VMEM((9, 2, crow, ccol), f32),
            pltpu.VMEM((2, 2, 2 * crow, 2 * ccol), f32),
            pltpu.VMEM((4 * crow, cols + LANE), f32),
            pltpu.VMEM((crow, ccol), f32),
            pltpu.VMEM((crow, ccol), f32),
            pltpu.VMEM((cols, ccol), jnp.bfloat16),
            pltpu.VMEM((2 * ccol, cols + LANE), jnp.bfloat16),
            pltpu.SemaphoreType.DMA((8, 5)),
            pltpu.SemaphoreType.DMA((8, 5)),
            pltpu.SemaphoreType.DMA((5,)),
            pltpu.SemaphoreType.DMA((4,)),
        ],
        compiler_params=pltpu.CompilerParams(
            collective_id=0, has_side_effects=True
        ),
    )(level_weight, excess_weight, soil_weight, column_water, land_soil, terrain_class,
      surface_head, conductivity, active_mask, flow_code)


def solution(mesh):
    in_specs = (
        P("comp", None, "gy", "gx"),
        P("comp", "gy", "gx"),
        P(),
        P(),
        P(),
        P("gy", "gx"),
        P("comp", "gy", "gx"),
        P("comp", "gy", "gx"),
        P("comp", "gy", "gx"),
        P("comp", "gy", "gx"),
    )
    body = functools.partial(per_device, mesh.shape["gy"], mesh.shape["gx"])
    return jax.shard_map(
        body, mesh=mesh, in_specs=in_specs, out_specs=P("comp", "gy", "gx"), check_vma=False
    )
```

profile of v0, /device:TPU:0, one launch (start us, length us, event | category | flops | bytes accessed | tf_op | source)
XLA Modules:
  0.0 25.6 jit_solution(2913359261365609760)
XLA Ops:
  0.0 24.3 %shard_map.100 = f32[1,8,128]{2,1,0:T(8,128)} custom-call(f32[16]{0:T(128)} %lw.1, f32[16]{0:T(128)} %ewt.1, f32[16]{0:T(128)} %swt.1, f32[1,16,8,128]{3,2,1,0:T(8,128)} %water_in.1, f32[1,8,128]{2,1,0:T(8,128)} %soil_in.1, s32[80,1280]{1,0:T(8,128)} %terrain_in.1, f32[1,80,1280]{2,1,0:T(8,128)} %head_in.1, f32[1,80,1280]{2,1,0:T(8,128)} %cond_in.1, ...), custom_call_target="tpu_custom_call" | custom-call | tf_op jit(solution)/shard_map/pallas_call | solution.py:546
  24.3 1.3 %copy.12 = f32[1,8,128]{2,1,0:T(8,128)} copy(f32[1,8,128]{2,1,0:T(8,128)} %shard_map.100) | data formatting | bytes 8192
where the time goes:
time: 25.8 us; the launch traced here: 25.6 us
  Pallas kernels  24.3 us (94%)
  local copies, waits for them, and re-layouts  1.28 us (5%)
    pallas_call x1, Pallas kernels, per_device(): pl.pallas_call(functools.partial(kernel, ny, nx), out_shape=jax.ShapeDtyp...  24.3 us
    unnamed x1, local copies, waits for them, and re-layouts  1.28 us

commit v1 on v0

--- a/solution.py
+++ b/solution.py
@@ -48,10 +48,10 @@
 
 def kernel(
     ny, nx,
-    lw, ewt, swt, water_in, soil_in, terrain_in, head_in, cond_in, active_in, code_in,
+    lw_in, ewt_in, swt_in, water_in, soil_in, terrain_in, head_in, cond_in, active_in, code_in,
     out_ref,
     xi, xf, st, ps, wb, mb, pk, dg, mn, qb, qx, back_tx, back_rx, gather, spreadm,
-    send, recv, local, hop,
+    lw, ewt, swt, send, recv, local, hop, tab,
 ):
     group = lax.axis_index("comp")
     gy = lax.axis_index("gy")
@@ -129,6 +129,12 @@
     for d in range(8):
         greeted = greeted + exists(d).astype(jnp.int32)
 
+    tables = [
+        pltpu.make_async_copy(a, b, tab.at[k])
+        for k, (a, b) in enumerate(((lw_in, lw), (ewt_in, ewt), (swt_in, swt)))
+    ]
+    for load in tables:
+        load.start()
     terrain_load.start()
 
     @pl.when(group == 0)
@@ -141,6 +147,41 @@
         for load in route_loads:
             load.start()
 
+    R, AD, M0, M1, M2, M3, EW, HD, SO = range(9)
+    WN, WS, WW, WE, AA, B0, B1, B2, B3 = range(9, 18)
+    k10 = iota((LANE, ccol), 1) * AGG
+    j0 = iota((LANE, ccol), 0)
+
+    for c in range(tiles):
+        j = j0 + c * LANE
+        gather[c * LANE : (c + 1) * LANE, :] = jnp.where(
+            (j >= k10) & (j < k10 + AGG), 1.0, 0.0
+        ).astype(jnp.bfloat16)
+
+    @pl.when(group == 1)
+    def _():
+        kk = iota((2 * ccol, LANE), 0)
+        jj = iota((2 * ccol, LANE), 1)
+        for c in range(tiles):
+            j = jj + c * LANE
+            spreadm[:, c * LANE : (c + 1) * LANE] = jnp.where(
+                (j >= kk * AGG) & (j < kk * AGG + AGG), 1.0, 0.0
+            ).astype(jnp.bfloat16)
+        spreadm[:, cols:] = jnp.where(
+            ((jj < 64) & (kk == ccol)) | ((jj >= 64) & (kk == 2 * ccol - 1)), 1.0, 0.0
+        ).astype(jnp.bfloat16)
+
+        zero = jnp.zeros((SUB, LANE), jnp.float32)
+        for c in range(width):
+            for edge in (0, (bands + 1) * SUB):
+                for k in (R, M0, M1):
+                    st[k, c, edge : edge + SUB] = zero
+                for k in range(2):
+                    for p in range(2):
+                        ps[p, k, c, edge : edge + SUB] = zero
+
+    for load in tables:
+        load.wait()
     pl.semaphore_wait(barrier, greeted)
 
     def land_first(d):
@@ -184,15 +225,6 @@
     @pl.when(group == 1)
     def _():
         over(range(8), lambda d: start_all(route_sends(d)))
-
-    k10 = iota((LANE, ccol), 1) * AGG
-    j0 = iota((LANE, ccol), 0)
-
-    for c in range(tiles):
-        j = j0 + c * LANE
-        gather[c * LANE : (c + 1) * LANE, :] = jnp.where(
-            (j >= k10) & (j < k10 + AGG), 1.0, 0.0
-        ).astype(jnp.bfloat16)
 
     def means(first, second):
         parts = []
@@ -330,31 +362,9 @@
         back_send.wait_recv()
         out_ref[0] = back_rx[...] / divisor
 
-    R, AD, M0, M1, M2, M3, EW, HD, SO = range(9)
-    WN, WS, WW, WE, AA, B0, B1, B2, B3 = range(9, 18)
 
     @pl.when(group == 1)
     def _():
-        kk = iota((2 * ccol, LANE), 0)
-        jj = iota((2 * ccol, LANE), 1)
-        for c in range(tiles):
-            j = jj + c * LANE
-            spreadm[:, c * LANE : (c + 1) * LANE] = jnp.where(
-                (j >= kk * AGG) & (j < kk * AGG + AGG), 1.0, 0.0
-            ).astype(jnp.bfloat16)
-        spreadm[:, cols:] = jnp.where(
-            ((jj < 64) & (kk == ccol)) | ((jj >= 64) & (kk == 2 * ccol - 1)), 1.0, 0.0
-        ).astype(jnp.bfloat16)
-
-        zero = jnp.zeros((SUB, LANE), jnp.float32)
-        for c in range(width):
-            for edge in (0, (bands + 1) * SUB):
-                for k in (R, M0, M1):
-                    st[k, c, edge : edge + SUB] = zero
-                for k in range(2):
-                    for p in range(2):
-                        ps[p, k, c, edge : edge + SUB] = zero
-
         def prepare(t, c):
             r = pl.ds(t * SUB if isinstance(t, int) else pl.multiple_of(t * SUB, SUB), SUB)
             o = pl.ds(
@@ -542,11 +552,10 @@
     tall = rows + 4 * SUB
     f32, i32 = jnp.float32, jnp.int32
     any_spec = pl.BlockSpec(memory_space=pltpu.HBM)
-    smem = pl.BlockSpec(memory_space=pltpu.SMEM)
     return pl.pallas_call(
         functools.partial(kernel, ny, nx),
-        out_shape=jax.ShapeDtypeStruct((1, crow, ccol), f32),
-        in_specs=[smem] * 3 + [any_spec] * 7,
+        out_shape=pltpu.VMEM((1, crow, ccol), f32),
+        in_specs=[any_spec] * 10,
         out_specs=pl.BlockSpec(memory_space=pltpu.VMEM),
         scratch_shapes=[
             pltpu.VMEM((3, rows + 2 * SUB, cols + 2 * LANE), i32),
@@ -564,10 +573,14 @@
             pltpu.VMEM((crow, ccol), f32),
             pltpu.VMEM((cols, ccol), jnp.bfloat16),
             pltpu.VMEM((2 * ccol, cols + LANE), jnp.bfloat16),
+            pltpu.SMEM(level_weight.shape, f32),
+            pltpu.SMEM(excess_weight.shape, f32),
+            pltpu.SMEM(soil_weight.shape, f32),
             pltpu.SemaphoreType.DMA((8, 5)),
             pltpu.SemaphoreType.DMA((8, 5)),
             pltpu.SemaphoreType.DMA((5,)),
             pltpu.SemaphoreType.DMA((4,)),
+            pltpu.SemaphoreType.DMA((3,)),
         ],
         compiler_params=pltpu.CompilerParams(
             collective_id=0, has_side_effects=True

time: 25.8 us -> 23.8 us (0.922)
  Pallas kernels: 24.3 us -> 23.1 us
  local copies, waits for them, and re-layouts: 1.28 us -> 0.6 us
    pallas_call x1, Pallas kernels: 24.3 us -> 23.1 us  [per_device(): pl.pallas_call(functools.partial(kernel, ny, nx), out_shape=pltpu.VMEM((1...]
    unnamed x1, local copies, waits for them, and re-layouts: 1.28 us -> 0.6 us
where the time goes in v1:
time: 23.8 us; the launch traced here: 23.7 us
  Pallas kernels  23.1 us (97%)
  local copies, waits for them, and re-layouts  0.6 us (3%)
    pallas_call x1, Pallas kernels, per_device(): pl.pallas_call(functools.partial(kernel, ny, nx), out_shape=pltpu.VMEM((1...  23.1 us
    unnamed x1, local copies, waits for them, and re-layouts  0.6 us

profile of v1, /device:TPU:0, one launch (start us, length us, event | category | flops | bytes accessed | tf_op | source)
XLA Modules:
  0.0 23.7 jit_solution(12593650418822530864)
XLA Ops:
  0.0 23.1 %shard_map.100 = f32[1,8,128]{2,1,0:T(8,128)S(1)} custom-call(f32[16]{0:T(128)} %lw_in.1, f32[16]{0:T(128)} %ewt_in.1, f32[16]{0:T(128)} %swt_in.1, f32[1,16,8,128]{3,2,1,0:T(8,128)} %water_in.1, f32[1,8,128]{2,1,0:T(8,128)} %soil_in.1, s32[80,1280]{1,0:T(8,128)} %terrain_in.1, f32[1,80,1280]{2,1,0:T(8,128)} %head_in.1, f32[1,80,1280]{2,1,0:T(8,128)} %cond_in.1, ...), custom_call_target="tpu_custom_call" | custom-call | tf_op jit(solution)/shard_map/pallas_call | solution.py:555
  23.1 0.6 %copy.12 = f32[1,8,128]{2,1,0:T(8,128)} copy(f32[1,8,128]{2,1,0:T(8,128)S(1)} %shard_map.100) | data formatting | bytes 8192

commit v2 on v0

v2 whole, which is shorter than its diff:
```python
import functools

import jax
import jax.numpy as jnp
from jax import lax
from jax.experimental import pallas as pl
from jax.experimental.pallas import tpu as pltpu
from jax.sharding import PartitionSpec as P

AGG = 10
NSUB = 8
SWEEPS = 2

diffusion_rate = 0.2
infiltration_rate = 0.05
drainage_rate = 0.1
half_point = 0.1
evaporation_scale = 0.5

LANE = 128
SUB = 8
MESH = pl.DeviceIdType.MESH
DIRS = ((-1, 0), (1, 0), (0, -1), (0, 1), (-1, -1), (-1, 1), (1, -1), (1, 1))
N, S, W, E, NW, NE, SW, SE = range(8)
OPP = (S, N, E, W, SE, SW, NE, NW)

R, K, RI, AD, M0, M1, M2, M3, EW, HD, SO, A1 = range(12)
PLANES = 5
U, Y, Q = range(3)
FIELDS = 4


def iota(shape, dim):
    return lax.broadcasted_iota(jnp.int32, shape, dim)


def pick(table, classes):
    values = [table[k] for k in range(table.shape[0])]
    bit = 1
    while len(values) > 1:
        odd = (classes & bit) != 0
        values = [
            jnp.where(odd, values[k + 1], values[k]) for k in range(0, len(values), 2)
        ]
        bit *= 2
    return values[0]


def halves(x):
    high = x.astype(jnp.bfloat16)
    return high, (x - high.astype(jnp.float32)).astype(jnp.bfloat16)


def turn(x, shift):
    shift %= LANE
    return pltpu.roll(x, shift, 1) if shift else x


def kernel(
    ny, nx,
    lw_in, ewt_in, swt_in, water_in, soil_in, terrain_in, head_in, cond_in, active_in, code_in,
    out_ref,
    lw, ewt, swt, xi, act, xf, st, us, wb, mb, wp, wr, pk, pr, fq, fr, qb, back_tx, back_rx,
    gather, perm, planes, hs, hr, sums, sp, sr, cr, send, recv, local, hop,
):
    group = lax.axis_index("comp")
    gy = lax.axis_index("gy")
    gx = lax.axis_index("gx")
    rows, cols = terrain_in.shape
    lev = water_in.shape[1]
    crow, ccol = soil_in.shape[1], soil_in.shape[2]
    tiles = cols // LANE
    width = tiles + 1
    own_bands = rows // SUB
    bands = own_bands + 2

    lane = iota((SUB, LANE), 1)
    sub = iota((SUB, LANE), 0)
    left = lane < LANE // 2
    upper = sub < SUB // 2

    def exists(d):
        dy, dx = DIRS[d]
        return (gy + dy >= 0) & (gy + dy < ny) & (gx + dx >= 0) & (gx + dx < nx)

    def at(d):
        dy, dx = DIRS[d]
        return {"comp": group, "gy": gy + dy, "gx": gx + dx}

    partner = {"comp": 1 - group, "gy": gy, "gx": gx}

    def copy(src, dst, d, f):
        return pltpu.make_async_remote_copy(
            src_ref=src, dst_ref=dst, send_sem=send.at[d, f], recv_sem=recv.at[OPP[d], f],
            device_id=at(d), device_id_type=MESH,
        )

    def arrival(dst, d, f):
        return pltpu.make_async_remote_copy(
            src_ref=dst, dst_ref=dst, send_sem=send.at[d, f], recv_sem=recv.at[d, f],
            device_id=at(d), device_id_type=MESH,
        )

    def across(src, dst, k):
        return pltpu.make_async_remote_copy(
            src_ref=src, dst_ref=dst, send_sem=hop.at[2 * k], recv_sem=hop.at[2 * k + 1],
            device_id=partner, device_id_type=MESH,
        )

    def over(dirs, action):
        for d in dirs:
            @pl.when(exists(d))
            def _():
                action(d)

    def load(src, dst, k):
        return pltpu.make_async_copy(src, dst, local.at[k])

    tables = [load(a, b, k) for k, (a, b) in enumerate(((lw_in, lw), (ewt_in, ewt), (swt_in, swt)))]
    terrain_load = load(terrain_in, xi.at[0], 3)
    land_loads = [load(water_in.at[0], wb, 4), load(soil_in.at[0], mb, 5)]
    route_loads = [
        load(cond_in.at[0], xf.at[0], 4),
        load(active_in.at[0], act, 5),
        load(code_in.at[0], xi.at[1], 6),
        load(head_in.at[0], xf.at[1], 7),
    ]

    barrier = pltpu.get_barrier_semaphore()
    greeted = 1
    for d in range(8):
        meet = exists(d) if d < 4 else exists(d) & (group == 0)
        greeted = greeted + meet.astype(jnp.int32)

        @pl.when(meet)
        def _():
            pl.semaphore_signal(barrier, inc=1, device_id=at(d), device_id_type=MESH)
    pl.semaphore_signal(barrier, inc=1, device_id=partner, device_id_type=MESH)

    for c in tables:
        c.start()

    @pl.when(group == 0)
    def _():
        terrain_load.start()
        for c in land_loads:
            c.start()

    @pl.when(group == 1)
    def _():
        for c in route_loads:
            c.start()
        terrain_load.start()

    def land_sends(d):
        if d < 2:
            return [copy(wp.at[d], wr.at[OPP[d]], d, 0), copy(fq, fr.at[OPP[d]], d, 1)]
        return [copy(pk.at[0 if DIRS[d][1] < 0 else 1], pr.at[OPP[d]], d, 0)]

    def land_arrivals(d):
        if d < 2:
            return [arrival(wr.at[d], d, 0), arrival(fr.at[d], d, 1)]
        return [arrival(pr.at[d], d, 0)]

    def route_sends(d):
        if d < 2:
            return [copy(hs.at[d], hr.at[OPP[d]], d, 0)]
        return [copy(sp.at[d - 2], sr.at[OPP[d] - 2], d, 0)]

    def route_arrivals(d):
        return [arrival(hr.at[d] if d < 2 else sr.at[d - 2], d, 0)]

    def corner_send(d, s):
        return copy(sr.at[s, 0], cr.at[OPP[d], s], d, 1 + s)

    def corner_arrival(d, s):
        return arrival(cr.at[d, s], d, 1 + s)

    def corners(action):
        for d in (N, S):
            for s in (0, 1):
                @pl.when(exists(d) & exists(W + s))
                def _():
                    action(d, s)

    s_send = across(qb.at[1, 0], qb.at[1, 1], 0)
    e_send = across(qb.at[0, 0], qb.at[0, 1], 1)
    back_send = across(back_tx, back_rx, 2)

    def mean(field):
        parts = [halves(tile) for tile in field]
        stacked = jnp.concatenate(
            [jnp.concatenate([p[k] for p in parts], axis=1) for k in (0, 1)], axis=0
        )
        y = jnp.dot(stacked, gather[...], preferred_element_type=jnp.float32)
        return pool(y[:rows] + y[rows:], 1.0)

    def pool(z, scale):
        i10 = iota((crow, rows), 0) * AGG
        i = iota((crow, rows), 1)
        ones = jnp.where((i >= i10) & (i < i10 + AGG), 1.0, 0.0).astype(jnp.bfloat16)
        high, low = halves(z)
        return jnp.dot(
            jnp.concatenate([ones, ones], axis=1), jnp.concatenate([high, low], axis=0),
            preferred_element_type=jnp.float32,
        ) * (scale / (AGG * AGG))

    def unpack(east, west, g):
        return jnp.where(left, turn(east, -SUB * g), turn(west, -SUB * g - SUB))

    @pl.when(group == 0)
    def _():
        k10 = iota((LANE, ccol), 1) * AGG
        j0 = iota((LANE, ccol), 0)
        for c in range(tiles):
            j = j0 + c * LANE
            gather[c * LANE : (c + 1) * LANE, :] = jnp.where(
                (j >= k10) & (j < k10 + AGG), 1.0, 0.0
            ).astype(jnp.bfloat16)
        for c in land_loads:
            c.wait()
        packs = [jnp.zeros((SUB, LANE), jnp.float32)] * 2
        for l in range(lev):
            mine = (lane >= SUB * l) & (lane < SUB * l + SUB)
            w = wb[l]
            packs[0] = jnp.where(mine, turn(w, SUB * l), packs[0])
            packs[1] = jnp.where(mine, turn(w, SUB * l + SUB), packs[1])
        pk[0, 0] = packs[0]
        pk[1, 0] = packs[1]
        for i in range(lev // 2):
            a, b = wb[2 * i], wb[2 * i + 1]
            wp[N, i] = jnp.where(upper, a, pltpu.roll(b, SUB // 2, 0))
            wp[S, i] = jnp.where(upper, pltpu.roll(a, SUB // 2, 0), b)

        for c in tables:
            c.wait()
        terrain_load.wait()
        firsts, seconds = [], []
        for c in range(tiles):
            tc = xi[0, :, c * LANE : (c + 1) * LANE]
            firsts.append(pick(ewt, tc))
            seconds.append(pick(swt, tc))
        m = mb[...]
        mm = m * m
        own_f = mm / ((mm + half_point) * mean(firsts))
        own_q = m / mean(seconds)
        fq[0] = own_f
        fq[1] = own_q
        for side in range(2):
            a, b = turn(own_f, SUB * side), turn(own_q, SUB * side + SUB)
            pk[side, 1] = jnp.where(lane < SUB, a, b)

        pl.semaphore_wait(barrier, greeted)
        over((4, 5, 6, 7, 2, 3, 0, 1), lambda d: [c.start() for c in land_sends(d)])

        def valid(a, b):
            r = sub + (0 if a == 0 else jnp.where(upper, crow, -crow)) + gy * crow
            k = lane + (0 if b == 0 else jnp.where(left, ccol, -ccol)) + gx * ccol
            return (r >= 0) & (r < ny * crow) & (k >= 0) & (k < nx * ccol)

        ok = [[valid(a, b) for b in range(2)] for a in range(2)]
        over(range(8), lambda d: [c.wait_recv() for c in land_arrivals(d)])

        def joined(own, ns, k, g):
            ce = jnp.where(upper, pr[SE, k], pr[NE, k])
            cw = jnp.where(upper, pr[SW, k], pr[NW, k])
            t = [[own, unpack(pr[E, k], pr[W, k], g)], [ns, unpack(ce, cw, g)]]
            return [[jnp.where(ok[a][b], t[a][b], 0.0) for b in range(2)] for a in range(2)]

        ratio = [
            joined(fq[f], jnp.where(upper, fr[S, f], fr[N, f]), 1, f) for f in range(2)
        ]
        def hand(k, t):
            for a in range(2):
                edge = jnp.where(
                    left, jnp.broadcast_to(t[a][1][:, :1], (SUB, LANE)),
                    jnp.broadcast_to(t[a][1][:, LANE - 1 :], (SUB, LANE)),
                )
                for b, v in enumerate((t[a][0], edge)):
                    qb[k, 0, a * SUB : (a + 1) * SUB, b * LANE : (b + 1) * LANE] = v

        hand(1, ratio[1])
        s_send.start()

        def smooth(t):
            new = [[None, None], [None, None]]
            down = [[pltpu.roll(t[a][b], 1, 0) for b in range(2)] for a in range(2)]
            up = [[pltpu.roll(t[a][b], SUB - 1, 0) for b in range(2)] for a in range(2)]
            right = [[pltpu.roll(t[a][b], 1, 1) for b in range(2)] for a in range(2)]
            lft = [[pltpu.roll(t[a][b], LANE - 1, 1) for b in range(2)] for a in range(2)]
            for a in range(2):
                for b in range(2):
                    around = (
                        jnp.where(sub == 0, down[1 - a][b], down[a][b])
                        + jnp.where(sub == SUB - 1, up[1 - a][b], up[a][b])
                        + jnp.where(lane == 0, right[a][1 - b], right[a][b])
                        + jnp.where(lane == LANE - 1, lft[a][1 - b], lft[a][b])
                    )
                    value = t[a][b] + diffusion_rate * (around - 4.0 * t[a][b])
                    new[a][b] = jnp.where(ok[a][b], value, 0.0)
            return new

        precip = [[0.0, 0.0], [0.0, 0.0]]
        ground = None
        for l in range(lev):
            n, s = wr[N, l // 2], wr[S, l // 2]
            if l % 2 == 0:
                n = pltpu.roll(n, SUB // 2, 0)
            else:
                s = pltpu.roll(s, SUB // 2, 0)
            t = joined(wb[l], jnp.where(upper, s, n), 0, l)
            for _ in range(SWEEPS):
                t = smooth(t)
            if l == 0:
                ground = t[0][0]
            for a in range(2):
                for b in range(2):
                    precip[a][b] = precip[a][b] + lw[l] * t[a][b] * t[a][b]

        hand(0, [[precip[a][b] * ratio[0][a][b] for b in range(2)] for a in range(2)])
        e_send.start()
        divisor = 1.0 + evaporation_scale * ground * ground
        over(range(8), lambda d: [c.wait_send() for c in land_sends(d)])
        s_send.wait_send()
        e_send.wait_send()
        back_send.wait_recv()
        out_ref[0] = back_rx[...] / divisor

    @pl.when(group == 1)
    def _():
        at_c = iota((2 * SUB, LANE), 1) * AGG - iota((2 * SUB, LANE), 0)

        def place(k, carry):
            j = pl.multiple_of(k * 2 * SUB, 2 * SUB)
            for c in range(tiles):
                perm[pl.ds(j, 2 * SUB), c * LANE : (c + 1) * LANE] = jnp.where(
                    at_c == j - c, 1.0, 0.0
                ).astype(jnp.bfloat16)
            return carry

        lax.fori_loop(0, cols // (2 * SUB), place, 0, unroll=4)
        zero = jnp.zeros((SUB, LANE), jnp.float32)
        for c in range(width):
            for edge in (0, (bands + 1) * SUB):
                for k in (R, M0, M1):
                    st[k, c, edge : edge + SUB] = zero
                for k in (U, Q):
                    for p in range(2):
                        us[p, k, c, edge : edge + SUB] = zero

        for c in route_loads:
            c.wait()
        terrain_load.wait()

        def stage(keff, code, head, tc):
            mixed = (code + 4 * tc).astype(jnp.float32).astype(jnp.bfloat16)
            return [mixed, *halves(keff), *halves(head)]

        def unmix(v, m, k, cs):
            got = [v[p * m + k : p * m + k + SUB, cs] for p in range(PLANES)]
            mixed = got[0].astype(jnp.int32)
            return got[1] + got[2], mixed & 3, got[3] + got[4], mixed >> 2

        chunk = 2 * LANE
        ends = (0, rows - SUB)

        def both(ref, *lead):
            return jnp.concatenate([ref[(*lead, slice(e, e + SUB))] for e in ends], axis=0)

        edge = jnp.concatenate(
            stage(both(xf, 0) * both(act).astype(jnp.float32), both(xi, 1), both(xf, 1), both(xi, 0)),
            axis=0,
        )
        for n in range(0, cols, chunk):
            v = jnp.dot(edge, perm[:, n : n + chunk], preferred_element_type=jnp.float32)
            for c in range(n // LANE, (n + chunk) // LANE):
                cs = slice(c * LANE - n, c * LANE - n + LANE)
                for d in (N, S):
                    for f, x in enumerate(unmix(v, 2 * SUB, d * SUB, cs)):
                        hs[d, f, c] = x.astype(jnp.float32)

        order = [0, own_bands - 1] + list(range(1, own_bands - 1))
        for side in range(2):
            cs = slice(0, LANE) if side == 0 else slice(cols - LANE, cols)
            for q in range(sp.shape[1]):
                tile = zero
                for i, b in enumerate(order[4 * q : 4 * q + 4]):
                    o = slice(b * SUB, b * SUB + SUB)
                    keff = xf[0, o, cs] * act[o, cs].astype(jnp.float32)
                    values = (
                        keff, xi[1, o, cs].astype(jnp.float32), xf[1, o, cs],
                        xi[0, o, cs].astype(jnp.float32),
                    )
                    for f, v in enumerate(values):
                        g = i * FIELDS + f
                        tile = jnp.where(
                            (lane >= SUB * g) & (lane < SUB * g + SUB),
                            turn(v, SUB * g + SUB * side), tile,
                        )
                sp[side, q] = tile

        pl.semaphore_wait(barrier, greeted)
        over((2, 3, 0, 1), lambda d: [c.start() for c in route_sends(d)])
        for c in tables:
            c.wait()

        def put(c, o, keff, head, code, tc):
            live = keff > 0.0
            rs = lax.rsqrt(jnp.where(live, keff, 1.0))
            r = keff * rs
            rate = jnp.where(live, drainage_rate * infiltration_rate, 0.0)
            st[R, c, o] = r
            st[K, c, o] = keff
            st[RI, c, o] = jnp.where(live, rs * (1.0 / infiltration_rate), 0.0)
            st[AD, c, o] = rate
            for k in range(4):
                st[M0 + k, c, o] = jnp.where(code == k, rate, 0.0)
            st[EW, c, o] = r * pick(ewt, tc)
            st[HD, c, o] = r * head
            st[SO, c, o] = pick(swt, tc) * (1.0 / infiltration_rate)

        def aligned(x):
            return x if isinstance(x, int) else pl.multiple_of(x, SUB)

        middle = rows - 2 * SUB
        for i in range(0, middle, 2 * SUB):
            o = slice(SUB + i, 3 * SUB + i)
            parts = stage(xf[0, o] * act[o].astype(jnp.float32), xi[1, o], xf[1, o], xi[0, o])
            for p, x in enumerate(parts):
                planes[p * middle + i : p * middle + i + 2 * SUB, :] = x
        for n in range(0, cols, chunk):
            v = jnp.dot(planes[...], perm[:, n : n + chunk], preferred_element_type=jnp.float32)
            for c in range(n // LANE, (n + chunk) // LANE):
                cs = slice(c * LANE - n, c * LANE - n + LANE)
                for t in range(2, bands - 2):
                    keff, code, head, tc = unmix(v, middle, (t - 2) * SUB, cs)
                    put(c, slice(t * SUB + SUB, t * SUB + 2 * SUB), keff, head, code, tc)

        def put_row(t, ref, d, there):
            for c in range(tiles):
                keff, code, head, tc = [
                    jnp.where((lane >= 0) & there, ref[d, f, c], 0.0) for f in range(FIELDS)
                ]
                put(c, slice(t * SUB + SUB, t * SUB + 2 * SUB), keff, head, code,
                    tc.astype(jnp.int32))

        yes = gy >= 0
        put_row(1, hs, N, yes)
        put_row(bands - 2, hs, S, yes)

        over((W, E), lambda d: [c.wait_recv() for c in route_arrivals(d)])
        corners(lambda d, s: corner_send(d, s).start())

        def side_ok(there):
            reach = (lane < SUB) & exists(E) | (lane >= LANE - SUB) & exists(W)
            return reach & there

        def put_side(t, east, west, g, there):
            ok = side_ok(there)
            keff, code, head, tc = [unpack(east, west, g + f) for f in range(FIELDS)]
            put(
                tiles, slice(t * SUB + SUB, t * SUB + 2 * SUB), jnp.where(ok, keff, 0.0),
                jnp.where(ok, head, 0.0), jnp.where(ok, code, 0.0),
                jnp.where(ok, tc, 0.0).astype(jnp.int32),
            )

        for i, b in enumerate(order):
            put_side(b + 1, sr[1, i // 4], sr[0, i // 4], (i % 4) * FIELDS, yes)

        def beside(west_of, east_of):
            w, e = west_of, east_of
            last = tiles - 1
            w_end, w_side = pltpu.roll(w[last], 1, 1), pltpu.roll(w[tiles], 1, 1)
            e_end, e_side = pltpu.roll(e[0], LANE - 1, 1), pltpu.roll(e[tiles], LANE - 1, 1)
            first, final = lane == 0, lane == LANE - 1
            west = [jnp.where(first, w_side, w_end), *w[:last], jnp.where(first, w_end, w_side)]
            east = [*e[1:tiles], jnp.where(final, e_side, e_end), jnp.where(final, e_end, e_side)]
            return west, east

        def around(t):
            base = aligned(t * SUB + SUB)
            return pl.ds(base, SUB), pl.ds(base - 1, SUB), pl.ds(base + 1, SUB)

        def couple(t, carry):
            o, above, below = around(t)
            r = [st[R, c, o] for c in range(width)]
            west, east = beside(r, r)
            for c in range(width):
                total = (st[R, c, above] + st[R, c, below]) + (west[c] + east[c])
                st[A1, c, o] = 1.0 - r[c] * total
            return carry

        lax.fori_loop(2, bands - 2, couple, 0, unroll=2)

        over((N, S), lambda d: [c.wait_recv() for c in route_arrivals(d)])
        corners(lambda d, s: corner_arrival(d, s).wait_recv())
        for t, d, g in ((0, N, FIELDS), (bands - 1, S, 0)):
            put_row(t, hr, d, exists(d))
            put_side(t, cr[d, 1], cr[d, 0], g, exists(d))
        for t in (0, 1, bands - 2, bands - 1):
            couple(t, 0)

        def up(k, t):
            if t == 0:
                a = b = 2 * crow - 1
            elif t == bands - 1:
                a = b = crow
            else:
                a, b = ((t - 1) * SUB) // AGG, ((t - 1) * SUB + SUB - 1) // AGG
            got = []
            for side in range(2):
                cs = slice(side * LANE, side * LANE + LANE)
                v = jnp.broadcast_to(qb[k, 1, a : a + 1, cs], (SUB, LANE))
                if a != b:
                    second = jnp.broadcast_to(qb[k, 1, b : b + 1, cs], (SUB, LANE))
                    v = jnp.where(sub < b * AGG - (t - 1) * SUB, v, second)
                got.append(v)
            return [got[0]] * tiles + [got[1]]

        s_send.wait_recv()
        for t in range(bands):
            o = slice((t + 1) * SUB, (t + 2) * SUB)
            for c, v in enumerate(up(1, t)):
                y = st[SO, c, o] * v
                us[0, Y, c, o] = y
                us[0, Q, c, o] = y * y

        e_send.wait_recv()
        for t in range(bands):
            o = slice((t + 1) * SUB, (t + 2) * SUB)
            for c, v in enumerate(up(0, t)):
                us[0, U, c, o] = st[HD, c, o] + st[EW, c, o] * v

        full = 1.0 / infiltration_rate

        def flows(src, o):
            q = [us[src, Q, c, o] for c in range(width)]
            return beside(
                [st[M3, c, o] * q[c] for c in range(width)],
                [st[M2, c, o] * q[c] for c in range(width)],
            )

        def soak(src, c, o):
            return us[src, U, c, o] * pl.reciprocal(us[src, Y, c, o] + full)

        def new_y(src, c, o, above, below, gu, sides):
            return (
                (us[src, Y, c, o] + st[RI, c, o] * gu)
                + (st[M0, c, below] * us[src, Q, c, below] + st[M1, c, above] * us[src, Q, c, above])
                + ((sides[0][c] + sides[1][c]) - st[AD, c, o] * us[src, Q, c, o])
            )

        def new_u(src, c, o, above, below, gu, sides):
            total = (us[src, U, c, above] + us[src, U, c, below]) + (sides[0][c] + sides[1][c])
            return (st[A1, c, o] * us[src, U, c, o] - gu) + st[K, c, o] * total

        def sides_u(src, o):
            u = [us[src, U, c, o] for c in range(width)]
            return beside(u, u)

        def substep(src, dst):
            def band(t, carry):
                o, above, below = around(t)
                u_sides, q_sides = sides_u(src, o), flows(src, o)
                for c in range(width):
                    gu = soak(src, c, o)
                    y = new_y(src, c, o, above, below, gu, q_sides)
                    us[dst, U, c, o] = new_u(src, c, o, above, below, gu, u_sides)
                    us[dst, Y, c, o] = y
                    us[dst, Q, c, o] = y * y
                return carry

            lax.fori_loop(0, bands, band, 0, unroll=UNROLL)

        def two(k, carry):
            substep(0, 1)
            substep(1, 0)
            return carry

        lax.fori_loop(0, NSUB // 2 - 1, two, 0)
        substep(0, 1)

        def last_y(t, carry):
            o, above, below = around(t)
            q_sides = flows(1, o)
            total = None
            for c in range(tiles):
                y = new_y(1, c, o, above, below, soak(1, c, o), q_sides)
                total = y if total is None else total + y
            sums[0, pl.ds(aligned(t * SUB - SUB), SUB)] = total
            return carry

        def last_u(t, carry):
            o, above, below = around(t)
            u_sides = sides_u(1, o)
            total = None
            for c in range(tiles):
                p = new_u(1, c, o, above, below, soak(1, c, o), u_sides) * st[RI, c, o]
                total = p if total is None else total + p
            sums[1, pl.ds(aligned(t * SUB - SUB), SUB)] = total
            return carry

        lax.fori_loop(1, bands - 1, last_y, 0, unroll=True)
        back_tx[...] = pool(sums[0], infiltration_rate)
        back_send.start()
        lax.fori_loop(1, bands - 1, last_u, 0, unroll=True)
        out_ref[0] = pool(sums[1], infiltration_rate)
        over(range(4), lambda d: [c.wait_send() for c in route_sends(d)])
        corners(lambda d, s: corner_send(d, s).wait_send())
        back_send.wait_send()


UNROLL = 4


def per_device(ny, nx, column_water, land_soil, level_weight, excess_weight, soil_weight,
               terrain_class, surface_head, conductivity, active_mask, flow_code):
    rows, cols = terrain_class.shape
    lev = column_water.shape[1]
    crow, ccol = land_soil.shape[1:]
    wide = cols // LANE + 1
    tall = rows + 4 * SUB
    packs = -(-(rows // SUB) // 4)
    f32, i32, bf16 = jnp.float32, jnp.int32, jnp.bfloat16
    hbm = pl.BlockSpec(memory_space=pltpu.HBM)
    return pl.pallas_call(
        functools.partial(kernel, ny, nx),
        out_shape=pltpu.VMEM((1, crow, ccol), f32),
        in_specs=[hbm] * 10,
        out_specs=pl.BlockSpec(memory_space=pltpu.VMEM),
        scratch_shapes=[
            pltpu.SMEM(level_weight.shape, f32),
            pltpu.SMEM(excess_weight.shape, f32),
            pltpu.SMEM(soil_weight.shape, f32),
            pltpu.VMEM((2, rows, cols), i32),
            pltpu.VMEM((rows, cols), i32),
            pltpu.VMEM((2, rows, cols), f32),
            pltpu.VMEM((12, wide, tall, LANE), f32),
            pltpu.VMEM((2, 3, wide, tall, LANE), f32),
            pltpu.VMEM((lev, crow, ccol), f32),
            pltpu.VMEM((crow, ccol), f32),
            pltpu.VMEM((2, lev // 2, crow, ccol), f32),
            pltpu.VMEM((2, lev // 2, crow, ccol), f32),
            pltpu.VMEM((2, 2, crow, ccol), f32),
            pltpu.VMEM((8, 2, crow, ccol), f32),
            pltpu.VMEM((2, crow, ccol), f32),
            pltpu.VMEM((2, 2, crow, ccol), f32),
            pltpu.VMEM((2, 2, 2 * crow, 2 * ccol), f32),
            pltpu.VMEM((crow, ccol), f32),
            pltpu.VMEM((crow, ccol), f32),
            pltpu.VMEM((cols, ccol), bf16),
            pltpu.VMEM((cols, cols), bf16),
            pltpu.VMEM((PLANES * (rows - 2 * SUB), cols), bf16),
            pltpu.VMEM((2, FIELDS, wide - 1, SUB, LANE), f32),
            pltpu.VMEM((2, FIELDS, wide - 1, SUB, LANE), f32),
            pltpu.VMEM((2, rows, LANE), f32),
            pltpu.VMEM((2, packs, SUB, LANE), f32),
            pltpu.VMEM((2, packs, SUB, LANE), f32),
            pltpu.VMEM((2, 2, SUB, LANE), f32),
            pltpu.SemaphoreType.DMA((8, 3)),
            pltpu.SemaphoreType.DMA((8, 3)),
            pltpu.SemaphoreType.DMA((8,)),
            pltpu.SemaphoreType.DMA((6,)),
        ],
        compiler_params=pltpu.CompilerParams(
            collective_id=0, has_side_effects=True
        ),
    )(level_weight, excess_weight, soil_weight, column_water, land_soil, terrain_class,
      surface_head, conductivity, active_mask, flow_code)


def solution(mesh):
    in_specs = (
        P("comp", None, "gy", "gx"),
        P("comp", "gy", "gx"),
        P(),
        P(),
        P(),
        P("gy", "gx"),
        P("comp", "gy", "gx"),
        P("comp", "gy", "gx"),
        P("comp", "gy", "gx"),
        P("comp", "gy", "gx"),
    )
    body = functools.partial(per_device, mesh.shape["gy"], mesh.shape["gx"])
    return jax.shard_map(
        body, mesh=mesh, in_specs=in_specs, out_specs=P("comp", "gy", "gx"), check_vma=False
    )
```

time: 25.8 us -> 19.5 us (0.76)
  Pallas kernels: 24.3 us -> 18.7 us
  local copies, waits for them, and re-layouts: 1.28 us -> 0.6 us
    pallas_call x1, Pallas kernels: 24.3 us -> 18.7 us  [per_device(): pl.pallas_call(functools.partial(kernel, ny, nx), out_shape=pltpu.VMEM((1...]
    unnamed x1, local copies, waits for them, and re-layouts: 1.28 us -> 0.6 us
where the time goes in v2:
time: 19.5 us; the launch traced here: 19.3 us
  Pallas kernels  18.7 us (96%)
  local copies, waits for them, and re-layouts  0.6 us (3%)
    pallas_call x1, Pallas kernels, per_device(): pl.pallas_call(functools.partial(kernel, ny, nx), out_shape=pltpu.VMEM((1...  18.7 us
    unnamed x1, local copies, waits for them, and re-layouts  0.6 us

profile of v2, /device:TPU:0, one launch (start us, length us, event | category | flops | bytes accessed | tf_op | source)
XLA Modules:
  0.0 19.3 jit_solution(8843154674807316248)
XLA Ops:
  0.0 18.7 %shard_map.100 = f32[1,8,128]{2,1,0:T(8,128)S(1)} custom-call(f32[16]{0:T(128)} %lw_in.1, f32[16]{0:T(128)} %ewt_in.1, f32[16]{0:T(128)} %swt_in.1, f32[1,16,8,128]{3,2,1,0:T(8,128)} %water_in.1, f32[1,8,128]{2,1,0:T(8,128)} %soil_in.1, s32[80,1280]{1,0:T(8,128)} %terrain_in.1, f32[1,80,1280]{2,1,0:T(8,128)} %head_in.1, f32[1,80,1280]{2,1,0:T(8,128)} %cond_in.1, ...), custom_call_target="tpu_custom_call" | custom-call | tf_op jit(solution)/shard_map/pallas_call | solution.py:626
  18.7 0.6 %copy.12 = f32[1,8,128]{2,1,0:T(8,128)} copy(f32[1,8,128]{2,1,0:T(8,128)S(1)} %shard_map.100) | data formatting | bytes 8192

commit v3 on v2

--- a/solution.py
+++ b/solution.py
@@ -24,7 +24,7 @@
 N, S, W, E, NW, NE, SW, SE = range(8)
 OPP = (S, N, E, W, SE, SW, NE, NW)
 
-R, K, RI, AD, M0, M1, M2, M3, EW, HD, SO, A1 = range(12)
+R, K, RI, AD, M0, M1, M2, EW, HD, SO, A1 = range(11)
 PLANES = 5
 U, Y, Q = range(3)
 FIELDS = 4
@@ -34,16 +34,8 @@
     return lax.broadcasted_iota(jnp.int32, shape, dim)
 
 
-def pick(table, classes):
-    values = [table[k] for k in range(table.shape[0])]
-    bit = 1
-    while len(values) > 1:
-        odd = (classes & bit) != 0
-        values = [
-            jnp.where(odd, values[k + 1], values[k]) for k in range(0, len(values), 2)
-        ]
-        bit *= 2
-    return values[0]
+def pick(lanes, classes):
+    return jnp.take_along_axis(lanes, classes, axis=1, mode="promise_in_bounds")
 
 
 def halves(x):
@@ -107,6 +99,12 @@
             device_id=partner, device_id_type=MESH,
         )
 
+    def spread_table(table):
+        v = jnp.zeros((SUB, LANE), jnp.float32)
+        for k in range(table.shape[0]):
+            v = jnp.where(lane == k, table[k], v)
+        return v
+
     def over(dirs, action):
         for d in dirs:
             @pl.when(exists(d))
@@ -119,12 +117,17 @@
     tables = [load(a, b, k) for k, (a, b) in enumerate(((lw_in, lw), (ewt_in, ewt), (swt_in, swt)))]
     terrain_load = load(terrain_in, xi.at[0], 3)
     land_loads = [load(water_in.at[0], wb, 4), load(soil_in.at[0], mb, 5)]
-    route_loads = [
-        load(cond_in.at[0], xf.at[0], 4),
-        load(active_in.at[0], act, 5),
-        load(code_in.at[0], xi.at[1], 6),
-        load(head_in.at[0], xf.at[1], 7),
+    ends = (0, rows - SUB)
+    bulk = [
+        (cond_in.at[0], xf.at[0]), (active_in.at[0], act), (code_in.at[0], xi.at[1]),
+        (head_in.at[0], xf.at[1]), (terrain_in, xi.at[0]),
     ]
+
+    def some(refs, start, size, k):
+        return load(*[r.at[pl.ds(start, size)] for r in refs], k)
+
+    edges = [some(r, e, SUB, 3 + 2 * k + i) for k, r in enumerate(bulk) for i, e in enumerate(ends)]
+    rest = [some(r, SUB, rows - 2 * SUB, 13 + k) for k, r in enumerate(bulk)]
 
     barrier = pltpu.get_barrier_semaphore()
     greeted = 1
@@ -137,30 +140,30 @@
             pl.semaphore_signal(barrier, inc=1, device_id=at(d), device_id_type=MESH)
     pl.semaphore_signal(barrier, inc=1, device_id=partner, device_id_type=MESH)
 
+    @pl.when(group == 0)
+    def _():
+        for c in land_loads:
+            c.start()
+        terrain_load.start()
+
+    @pl.when(group == 1)
+    def _():
+        for c in edges + rest:
+            c.start()
+
     for c in tables:
         c.start()
-
-    @pl.when(group == 0)
-    def _():
-        terrain_load.start()
-        for c in land_loads:
-            c.start()
-
-    @pl.when(group == 1)
-    def _():
-        for c in route_loads:
-            c.start()
-        terrain_load.start()
 
     def land_sends(d):
         if d < 2:
             return [copy(wp.at[d], wr.at[OPP[d]], d, 0), copy(fq, fr.at[OPP[d]], d, 1)]
-        return [copy(pk.at[0 if DIRS[d][1] < 0 else 1], pr.at[OPP[d]], d, 0)]
+        side = 0 if DIRS[d][1] < 0 else 1
+        return [copy(pk.at[side, k], pr.at[OPP[d], k], d, k) for k in range(2)]
 
     def land_arrivals(d):
         if d < 2:
             return [arrival(wr.at[d], d, 0), arrival(fr.at[d], d, 1)]
-        return [arrival(pr.at[d], d, 0)]
+        return [arrival(pr.at[d, k], d, k) for k in range(2)]
 
     def route_sends(d):
         if d < 2:
@@ -183,40 +186,39 @@
                 def _():
                     action(d, s)
 
-    s_send = across(qb.at[1, 0], qb.at[1, 1], 0)
+    s_send = across(qb.at[1, 0, pl.ds(0, SUB)], qb.at[1, 1, pl.ds(0, SUB)], 0)
     e_send = across(qb.at[0, 0], qb.at[0, 1], 1)
     back_send = across(back_tx, back_rx, 2)
 
-    def mean(field):
-        parts = [halves(tile) for tile in field]
-        stacked = jnp.concatenate(
-            [jnp.concatenate([p[k] for p in parts], axis=1) for k in (0, 1)], axis=0
-        )
-        y = jnp.dot(stacked, gather[...], preferred_element_type=jnp.float32)
-        return pool(y[:rows] + y[rows:], 1.0)
-
-    def pool(z, scale):
+    def pool_rows():
         i10 = iota((crow, rows), 0) * AGG
         i = iota((crow, rows), 1)
         ones = jnp.where((i >= i10) & (i < i10 + AGG), 1.0, 0.0).astype(jnp.bfloat16)
-        high, low = halves(z)
+        return jnp.concatenate([ones, ones], axis=1)
+
+    def pool(z, scale):
         return jnp.dot(
-            jnp.concatenate([ones, ones], axis=1), jnp.concatenate([high, low], axis=0),
-            preferred_element_type=jnp.float32,
+            pool_rows(), jnp.concatenate(halves(z), axis=0), preferred_element_type=jnp.float32
         ) * (scale / (AGG * AGG))
+
+    def block_means(fields):
+        ones = pool_rows()
+        summed = []
+        for field in fields:
+            parts = [jnp.concatenate(halves(tile), axis=0) for tile in field]
+            summed.append(
+                jnp.dot(ones, jnp.concatenate(parts, axis=1), preferred_element_type=jnp.float32)
+            )
+        stacked = jnp.concatenate(halves(jnp.concatenate(summed, axis=0)), axis=0)
+        y = jnp.dot(stacked, gather[...], preferred_element_type=jnp.float32)
+        total = (y[: 2 * crow] + y[2 * crow :]) * (1.0 / (AGG * AGG))
+        return total[:crow], total[crow:]
 
     def unpack(east, west, g):
         return jnp.where(left, turn(east, -SUB * g), turn(west, -SUB * g - SUB))
 
     @pl.when(group == 0)
     def _():
-        k10 = iota((LANE, ccol), 1) * AGG
-        j0 = iota((LANE, ccol), 0)
-        for c in range(tiles):
-            j = j0 + c * LANE
-            gather[c * LANE : (c + 1) * LANE, :] = jnp.where(
-                (j >= k10) & (j < k10 + AGG), 1.0, 0.0
-            ).astype(jnp.bfloat16)
         for c in land_loads:
             c.wait()
         packs = [jnp.zeros((SUB, LANE), jnp.float32)] * 2
@@ -232,26 +234,38 @@
             wp[N, i] = jnp.where(upper, a, pltpu.roll(b, SUB // 2, 0))
             wp[S, i] = jnp.where(upper, pltpu.roll(a, SUB // 2, 0), b)
 
+        pl.semaphore_wait(barrier, greeted)
+        over((0, 1, 4, 5, 6, 7, 2, 3), lambda d: land_sends(d)[0].start())
+
+        k10 = iota((LANE, ccol), 1) * AGG
+        j0 = iota((LANE, ccol), 0)
+        for c in range(tiles):
+            j = j0 + c * LANE
+            gather[c * LANE : (c + 1) * LANE, :] = jnp.where(
+                (j >= k10) & (j < k10 + AGG), 1.0, 0.0
+            ).astype(jnp.bfloat16)
         for c in tables:
             c.wait()
         terrain_load.wait()
+        ew_lanes, sw_lanes = spread_table(ewt), spread_table(swt)
         firsts, seconds = [], []
         for c in range(tiles):
             tc = xi[0, :, c * LANE : (c + 1) * LANE]
-            firsts.append(pick(ewt, tc))
-            seconds.append(pick(swt, tc))
+            parts = [tc[i : i + SUB] for i in range(0, rows, SUB)]
+            firsts.append(jnp.concatenate([pick(ew_lanes, x) for x in parts], axis=0))
+            seconds.append(jnp.concatenate([pick(sw_lanes, x) for x in parts], axis=0))
         m = mb[...]
         mm = m * m
-        own_f = mm / ((mm + half_point) * mean(firsts))
-        own_q = m / mean(seconds)
+        mean_e, mean_s = block_means((firsts, seconds))
+        own_f = mm / ((mm + half_point) * mean_e)
+        own_q = m / mean_s
         fq[0] = own_f
         fq[1] = own_q
         for side in range(2):
             a, b = turn(own_f, SUB * side), turn(own_q, SUB * side + SUB)
             pk[side, 1] = jnp.where(lane < SUB, a, b)
 
-        pl.semaphore_wait(barrier, greeted)
-        over((4, 5, 6, 7, 2, 3, 0, 1), lambda d: [c.start() for c in land_sends(d)])
+        over((4, 5, 6, 7, 0, 1, 2, 3), lambda d: land_sends(d)[1].start())
 
         def valid(a, b):
             r = sub + (0 if a == 0 else jnp.where(upper, crow, -crow)) + gy * crow
@@ -259,28 +273,13 @@
             return (r >= 0) & (r < ny * crow) & (k >= 0) & (k < nx * ccol)
 
         ok = [[valid(a, b) for b in range(2)] for a in range(2)]
-        over(range(8), lambda d: [c.wait_recv() for c in land_arrivals(d)])
+        over(range(8), lambda d: land_arrivals(d)[0].wait_recv())
 
         def joined(own, ns, k, g):
             ce = jnp.where(upper, pr[SE, k], pr[NE, k])
             cw = jnp.where(upper, pr[SW, k], pr[NW, k])
             t = [[own, unpack(pr[E, k], pr[W, k], g)], [ns, unpack(ce, cw, g)]]
             return [[jnp.where(ok[a][b], t[a][b], 0.0) for b in range(2)] for a in range(2)]
-
-        ratio = [
-            joined(fq[f], jnp.where(upper, fr[S, f], fr[N, f]), 1, f) for f in range(2)
-        ]
-        def hand(k, t):
-            for a in range(2):
-                edge = jnp.where(
-                    left, jnp.broadcast_to(t[a][1][:, :1], (SUB, LANE)),
-                    jnp.broadcast_to(t[a][1][:, LANE - 1 :], (SUB, LANE)),
-                )
-                for b, v in enumerate((t[a][0], edge)):
-                    qb[k, 0, a * SUB : (a + 1) * SUB, b * LANE : (b + 1) * LANE] = v
-
-        hand(1, ratio[1])
-        s_send.start()
 
         def smooth(t):
             new = [[None, None], [None, None]]
@@ -317,7 +316,28 @@
                 for b in range(2):
                     precip[a][b] = precip[a][b] + lw[l] * t[a][b] * t[a][b]
 
-        hand(0, [[precip[a][b] * ratio[0][a][b] for b in range(2)] for a in range(2)])
+        def ends(t):
+            edge = jnp.where(
+                left, jnp.broadcast_to(t[1][:, :1], (SUB, LANE)),
+                jnp.broadcast_to(t[1][:, LANE - 1 :], (SUB, LANE)),
+            )
+            return [t[0], edge]
+
+        over(range(8), lambda d: land_arrivals(d)[1].wait_recv())
+        ratio = [
+            joined(fq[f], jnp.where(upper, fr[S, f], fr[N, f]), 1, f) for f in range(2)
+        ]
+        for b, v in enumerate(ends(ratio[1][0])):
+            qb[1, 0, :SUB, b * LANE : (b + 1) * LANE] = v
+        s_send.start()
+        own, ring = [
+            ends([precip[a][b] * ratio[0][a][b] for b in range(2)]) for a in range(2)
+        ]
+        for b, v in enumerate(ends(ratio[1][1])):
+            cs = slice(b * LANE, (b + 1) * LANE)
+            qb[0, 0, :SUB, cs] = own[b]
+            v = jnp.where(sub == 1, pltpu.roll(v, 1, 0), pltpu.roll(v, SUB - 1, 0))
+            qb[0, 0, SUB:, cs] = jnp.where((sub == 1) | (sub == SUB - 2), v, ring[b])
         e_send.start()
         divisor = 1.0 + evaporation_scale * ground * ground
         over(range(8), lambda d: [c.wait_send() for c in land_sends(d)])
@@ -328,17 +348,18 @@
 
     @pl.when(group == 1)
     def _():
-        at_c = iota((2 * SUB, LANE), 1) * AGG - iota((2 * SUB, LANE), 0)
-
-        def place(k, carry):
+        at_c = (iota((2 * SUB, LANE), 1) * AGG - iota((2 * SUB, LANE), 0)).astype(jnp.int16)
+        one, none = jnp.ones((2 * SUB, LANE), jnp.bfloat16), jnp.zeros((2 * SUB, LANE), jnp.bfloat16)
+
+        def place(k, at):
             j = pl.multiple_of(k * 2 * SUB, 2 * SUB)
             for c in range(tiles):
                 perm[pl.ds(j, 2 * SUB), c * LANE : (c + 1) * LANE] = jnp.where(
-                    at_c == j - c, 1.0, 0.0
-                ).astype(jnp.bfloat16)
-            return carry
-
-        lax.fori_loop(0, cols // (2 * SUB), place, 0, unroll=4)
+                    at == jnp.int16(-c), one, none
+                )
+            return at - jnp.int16(2 * SUB)
+
+        lax.fori_loop(0, cols // (2 * SUB), place, at_c, unroll=4)
         zero = jnp.zeros((SUB, LANE), jnp.float32)
         for c in range(width):
             for edge in (0, (bands + 1) * SUB):
@@ -348,9 +369,8 @@
                     for p in range(2):
                         us[p, k, c, edge : edge + SUB] = zero
 
-        for c in route_loads:
+        for c in edges:
             c.wait()
-        terrain_load.wait()
 
         def stage(keff, code, head, tc):
             mixed = (code + 4 * tc).astype(jnp.float32).astype(jnp.bfloat16)
@@ -362,8 +382,6 @@
             return got[1] + got[2], mixed & 3, got[3] + got[4], mixed >> 2
 
         chunk = 2 * LANE
-        ends = (0, rows - SUB)
-
         def both(ref, *lead):
             return jnp.concatenate([ref[(*lead, slice(e, e + SUB))] for e in ends], axis=0)
 
@@ -379,6 +397,10 @@
                     for f, x in enumerate(unmix(v, 2 * SUB, d * SUB, cs)):
                         hs[d, f, c] = x.astype(jnp.float32)
 
+        pl.semaphore_wait(barrier, greeted)
+        over((0, 1), lambda d: [c.start() for c in route_sends(d)])
+        for c in rest:
+            c.wait()
         order = [0, own_bands - 1] + list(range(1, own_bands - 1))
         for side in range(2):
             cs = slice(0, LANE) if side == 0 else slice(cols - LANE, cols)
@@ -399,10 +421,10 @@
                         )
                 sp[side, q] = tile
 
-        pl.semaphore_wait(barrier, greeted)
-        over((2, 3, 0, 1), lambda d: [c.start() for c in route_sends(d)])
+        over((2, 3), lambda d: [c.start() for c in route_sends(d)])
         for c in tables:
             c.wait()
+        ew_lanes, sw_lanes = spread_table(ewt), spread_table(swt)
 
         def put(c, o, keff, head, code, tc):
             live = keff > 0.0
@@ -413,11 +435,12 @@
             st[K, c, o] = keff
             st[RI, c, o] = jnp.where(live, rs * (1.0 / infiltration_rate), 0.0)
             st[AD, c, o] = rate
-            for k in range(4):
-                st[M0 + k, c, o] = jnp.where(code == k, rate, 0.0)
-            st[EW, c, o] = r * pick(ewt, tc)
+            st[M0, c, o] = jnp.where(code == 0, rate, 0.0)
+            st[M1, c, o] = jnp.where(code == 1, rate, 0.0)
+            st[M2, c, o] = jnp.where(code == 2, rate, jnp.where(code == 3, -rate, 0.0))
+            st[EW, c, o] = r * pick(ew_lanes, tc)
             st[HD, c, o] = r * head
-            st[SO, c, o] = pick(swt, tc) * (1.0 / infiltration_rate)
+            st[SO, c, o] = pick(sw_lanes, tc) * (1.0 / infiltration_rate)
 
         def aligned(x):
             return x if isinstance(x, int) else pl.multiple_of(x, SUB)
@@ -501,31 +524,37 @@
             couple(t, 0)
 
         def up(k, t):
+            ring = 0 if t in (0, bands - 1) else k
             if t == 0:
-                a = b = 2 * crow - 1
+                a = b = 2 * crow - 1 - k
             elif t == bands - 1:
-                a = b = crow
+                a = b = crow + k
             else:
                 a, b = ((t - 1) * SUB) // AGG, ((t - 1) * SUB + SUB - 1) // AGG
             got = []
             for side in range(2):
                 cs = slice(side * LANE, side * LANE + LANE)
-                v = jnp.broadcast_to(qb[k, 1, a : a + 1, cs], (SUB, LANE))
+                v = jnp.broadcast_to(qb[ring, 1, a : a + 1, cs], (SUB, LANE))
                 if a != b:
-                    second = jnp.broadcast_to(qb[k, 1, b : b + 1, cs], (SUB, LANE))
+                    second = jnp.broadcast_to(qb[ring, 1, b : b + 1, cs], (SUB, LANE))
                     v = jnp.where(sub < b * AGG - (t - 1) * SUB, v, second)
                 got.append(v)
             return [got[0]] * tiles + [got[1]]
 
-        s_send.wait_recv()
-        for t in range(bands):
+        def start_y(t):
             o = slice((t + 1) * SUB, (t + 2) * SUB)
             for c, v in enumerate(up(1, t)):
                 y = st[SO, c, o] * v
                 us[0, Y, c, o] = y
                 us[0, Q, c, o] = y * y
 
+        s_send.wait_recv()
+        for t in range(1, bands - 1):
+            start_y(t)
+
         e_send.wait_recv()
+        start_y(0)
+        start_y(bands - 1)
         for t in range(bands):
             o = slice((t + 1) * SUB, (t + 2) * SUB)
             for c, v in enumerate(up(0, t)):
@@ -533,39 +562,74 @@
 
         full = 1.0 / infiltration_rate
 
-        def flows(src, o):
-            q = [us[src, Q, c, o] for c in range(width)]
-            return beside(
-                [st[M3, c, o] * q[c] for c in range(width)],
-                [st[M2, c, o] * q[c] for c in range(width)],
+        def flows(q, o):
+            h = [st[M2, c, o] * q[c] for c in range(width)]
+            west, east = beside(h, h)
+            return [
+                jnp.maximum(east[c], 0.0) - jnp.minimum(west[c], 0.0) for c in range(width)
+            ]
+
+        def sums_u(u):
+            west, east = beside(u, u)
+            return [west[c] + east[c] for c in range(width)]
+
+        def new_y(src, c, o, above, below, y, q, gu, side):
+            return (
+                (y + st[RI, c, o] * gu)
+                + (st[M0, c, below] * us[src, Q, c, below] + st[M1, c, above] * us[src, Q, c, above])
+                + (side - st[AD, c, o] * q)
             )
 
-        def soak(src, c, o):
-            return us[src, U, c, o] * pl.reciprocal(us[src, Y, c, o] + full)
-
-        def new_y(src, c, o, above, below, gu, sides):
-            return (
-                (us[src, Y, c, o] + st[RI, c, o] * gu)
-                + (st[M0, c, below] * us[src, Q, c, below] + st[M1, c, above] * us[src, Q, c, above])
-                + ((sides[0][c] + sides[1][c]) - st[AD, c, o] * us[src, Q, c, o])
-            )
-
-        def new_u(src, c, o, above, below, gu, sides):
-            total = (us[src, U, c, above] + us[src, U, c, below]) + (sides[0][c] + sides[1][c])
-            return (st[A1, c, o] * us[src, U, c, o] - gu) + st[K, c, o] * total
-
-        def sides_u(src, o):
-            u = [us[src, U, c, o] for c in range(width)]
-            return beside(u, u)
+        def new_u(src, c, o, above, below, u, gu, side):
+            total = (us[src, U, c, above] + us[src, U, c, below]) + side
+            return (st[A1, c, o] * u - gu) + st[K, c, o] * total
+
+        def held(src, k, o):
+            return [us[src, k, c, o] for c in range(width)]
 
         def substep(src, dst):
             def band(t, carry):
                 o, above, below = around(t)
-                u_sides, q_sides = sides_u(src, o), flows(src, o)
-                for c in range(width):
-                    gu = soak(src, c, o)
-                    y = new_y(src, c, o, above, below, gu, q_sides)
-                    us[dst, U, c, o] = new_u(src, c, o, above, below, gu, u_sides)
+                last = tiles - 1
+
+                def get_u(c):
+                    return us[src, U, c, o]
+
+                def get_h(c):
+                    return st[M2, c, o] * us[src, Q, c, o]
+
+                ends = []
+                for get in (get_u, get_h):
+                    w_end, w_side = pltpu.roll(get(last), 1, 1), pltpu.roll(get(tiles), 1, 1)
+                    e_end, e_side = (
+                        pltpu.roll(get(0), LANE - 1, 1), pltpu.roll(get(tiles), LANE - 1, 1)
+                    )
+                    ends.append((w_end, w_side, e_end, e_side))
+                first, final = lane == 0, lane == LANE - 1
+                u, h = {}, {}
+                for c in [*range(1, width), 0]:
+                    for k in (c - 1, c, c + 1):
+                        if k in range(width) and (c not in (0, tiles) or k == c) and k not in u:
+                            u[k], h[k] = get_u(k), get_h(k)
+                    west, east = [], []
+                    for near, (w_end, w_side, e_end, e_side) in zip((u, h), ends):
+                        if c == 0:
+                            west.append(jnp.where(first, w_side, w_end))
+                        elif c == tiles:
+                            west.append(jnp.where(first, w_end, w_side))
+                        else:
+                            west.append(near[c - 1])
+                        if c == last:
+                            east.append(jnp.where(final, e_side, e_end))
+                        elif c == tiles:
+                            east.append(jnp.where(final, e_end, e_side))
+                        else:
+                            east.append(near[c + 1])
+                    y = us[src, Y, c, o]
+                    gu = u[c] * pl.reciprocal(y + full)
+                    side = jnp.maximum(east[1], 0.0) - jnp.minimum(west[1], 0.0)
+                    us[dst, U, c, o] = new_u(src, c, o, above, below, u[c], gu, west[0] + east[0])
+                    y = new_y(src, c, o, above, below, y, us[src, Q, c, o], gu, side)
                     us[dst, Y, c, o] = y
                     us[dst, Q, c, o] = y * y
                 return carry
@@ -582,20 +646,25 @@
 
         def last_y(t, carry):
             o, above, below = around(t)
-            q_sides = flows(1, o)
+            u, q = held(1, U, o), held(1, Q, o)
+            q_sides = flows(q, o)
             total = None
             for c in range(tiles):
-                y = new_y(1, c, o, above, below, soak(1, c, o), q_sides)
+                y = us[1, Y, c, o]
+                gu = u[c] * pl.reciprocal(y + full)
+                y = new_y(1, c, o, above, below, y, q[c], gu, q_sides[c])
                 total = y if total is None else total + y
             sums[0, pl.ds(aligned(t * SUB - SUB), SUB)] = total
             return carry
 
         def last_u(t, carry):
             o, above, below = around(t)
-            u_sides = sides_u(1, o)
+            u = held(1, U, o)
+            u_sides = sums_u(u)
             total = None
             for c in range(tiles):
-                p = new_u(1, c, o, above, below, soak(1, c, o), u_sides) * st[RI, c, o]
+                gu = u[c] * pl.reciprocal(us[1, Y, c, o] + full)
+                p = new_u(1, c, o, above, below, u[c], gu, u_sides[c]) * st[RI, c, o]
                 total = p if total is None else total + p
             sums[1, pl.ds(aligned(t * SUB - SUB), SUB)] = total
             return carry
@@ -610,7 +679,7 @@
         back_send.wait_send()
 
 
-UNROLL = 4
+UNROLL = 12
 
 
 def per_device(ny, nx, column_water, land_soil, level_weight, excess_weight, soil_weight,
@@ -635,7 +704,7 @@
             pltpu.VMEM((2, rows, cols), i32),
             pltpu.VMEM((rows, cols), i32),
             pltpu.VMEM((2, rows, cols), f32),
-            pltpu.VMEM((12, wide, tall, LANE), f32),
+            pltpu.VMEM((11, wide, tall, LANE), f32),
             pltpu.VMEM((2, 3, wide, tall, LANE), f32),
             pltpu.VMEM((lev, crow, ccol), f32),
             pltpu.VMEM((crow, ccol), f32),
@@ -659,7 +728,7 @@
             pltpu.VMEM((2, 2, SUB, LANE), f32),
             pltpu.SemaphoreType.DMA((8, 3)),
             pltpu.SemaphoreType.DMA((8, 3)),
-            pltpu.SemaphoreType.DMA((8,)),
+            pltpu.SemaphoreType.DMA((18,)),
             pltpu.SemaphoreType.DMA((6,)),
         ],
         compiler_params=pltpu.CompilerParams(

time: 19.5 us -> 19.2 us (0.985)
  Pallas kernels: 18.7 us -> 18.4 us
    pallas_call x1, Pallas kernels: 18.7 us -> 18.4 us  [per_device(): pl.pallas_call(functools.partial(kernel, ny, nx), out_shape=pltpu.VMEM((1...]
where the time goes in v3:
time: 19.2 us; the launch traced here: 19 us
  Pallas kernels  18.4 us (96%)
  local copies, waits for them, and re-layouts  0.6 us (3%)
    pallas_call x1, Pallas kernels, per_device(): pl.pallas_call(functools.partial(kernel, ny, nx), out_shape=pltpu.VMEM((1...  18.4 us
    unnamed x1, local copies, waits for them, and re-layouts  0.6 us

profile of v3, /device:TPU:0, one launch (start us, length us, event | category | flops | bytes accessed | tf_op | source)
XLA Modules:
  0.0 19.0 jit_solution(9858397147243929823)
XLA Ops:
  0.0 18.4 %shard_map.100 = f32[1,8,128]{2,1,0:T(8,128)S(1)} custom-call(f32[16]{0:T(128)} %lw_in.1, f32[16]{0:T(128)} %ewt_in.1, f32[16]{0:T(128)} %swt_in.1, f32[1,16,8,128]{3,2,1,0:T(8,128)} %water_in.1, f32[1,8,128]{2,1,0:T(8,128)} %soil_in.1, s32[80,1280]{1,0:T(8,128)} %terrain_in.1, f32[1,80,1280]{2,1,0:T(8,128)} %head_in.1, f32[1,80,1280]{2,1,0:T(8,128)} %cond_in.1, ...), custom_call_target="tpu_custom_call" | custom-call | tf_op jit(solution)/shard_map/pallas_call | solution.py:695
  18.5 0.6 %copy.12 = f32[1,8,128]{2,1,0:T(8,128)} copy(f32[1,8,128]{2,1,0:T(8,128)S(1)} %shard_map.100) | data formatting | bytes 8192

commit v4 on v3

--- a/solution.py
+++ b/solution.py
@@ -235,7 +235,7 @@
             wp[S, i] = jnp.where(upper, pltpu.roll(a, SUB // 2, 0), b)
 
         pl.semaphore_wait(barrier, greeted)
-        over((0, 1, 4, 5, 6, 7, 2, 3), lambda d: land_sends(d)[0].start())
+        over((4, 5, 6, 7, 0, 1, 2, 3), lambda d: land_sends(d)[0].start())
 
         k10 = iota((LANE, ccol), 1) * AGG
         j0 = iota((LANE, ccol), 0)

time: 19.2 us -> 18.8 us (0.979)
  Pallas kernels: 18.4 us -> 18.1 us
    pallas_call x1, Pallas kernels: 18.4 us -> 18.1 us  [per_device(): pl.pallas_call(functools.partial(kernel, ny, nx), out_shape=pltpu.VMEM((1...]
where the time goes in v4:
time: 18.8 us; the launch traced here: 18.7 us
  Pallas kernels  18.1 us (96%)
  local copies, waits for them, and re-layouts  0.6 us (3%)
    pallas_call x1, Pallas kernels, per_device(): pl.pallas_call(functools.partial(kernel, ny, nx), out_shape=pltpu.VMEM((1...  18.1 us
    unnamed x1, local copies, waits for them, and re-layouts  0.6 us

profile of v4, /device:TPU:0, one launch (start us, length us, event | category | flops | bytes accessed | tf_op | source)
XLA Modules:
  0.0 18.7 jit_solution(4464023470183645933)
XLA Ops:
  0.0 18.1 %shard_map.100 = f32[1,8,128]{2,1,0:T(8,128)S(1)} custom-call(f32[16]{0:T(128)} %lw_in.1, f32[16]{0:T(128)} %ewt_in.1, f32[16]{0:T(128)} %swt_in.1, f32[1,16,8,128]{3,2,1,0:T(8,128)} %water_in.1, f32[1,8,128]{2,1,0:T(8,128)} %soil_in.1, s32[80,1280]{1,0:T(8,128)} %terrain_in.1, f32[1,80,1280]{2,1,0:T(8,128)} %head_in.1, f32[1,80,1280]{2,1,0:T(8,128)} %cond_in.1, ...), custom_call_target="tpu_custom_call" | custom-call | tf_op jit(solution)/shard_map/pallas_call | solution.py:695
  18.1 0.6 %copy.12 = f32[1,8,128]{2,1,0:T(8,128)} copy(f32[1,8,128]{2,1,0:T(8,128)S(1)} %shard_map.100) | data formatting | bytes 8192
